TPU v7x, 32 devices: a whole 2x2x4 slice. The times are simulated.
32 devices in a mesh: parts: 2 (over x), row: 16 (over z, y, core).
Axes of the slice: x: 2, y: 2, z: 4, core: 2. Of those that a mesh axis runs over, the one named last changes fastest.
Arguments:
- sigma_top: bfloat16 [4096, 2048], P(('parts', 'row')), parts along dimension 0, may hold values from -2 to 8, as said below
- panel_par: bfloat16 [4096, 1024], P(('parts', 'row')), parts along dimension 0, may hold values from -0.25 to 0.25
- dinv_par: float32 [2048, 1024], P(('parts', 'row')), parts along dimension 0, may hold values from -2 to 8, as said below
- panel_kid_top: bfloat16 [4, 2048, 1024], P('parts', 'row'), parts along dimension 0, may hold values from -0.25 to 0.25
- panel_kid_par: bfloat16 [4, 1024, 1024], P('parts', 'row'), parts along dimension 0, may hold values from -0.375 to 0.375
- dvar_kid: float32 [4, 1024], P('parts'), parts along dimension 0, may hold values from 0.5 to 2
- mask_par: int32 [16, 4], P('parts'), parts along dimension 0, may hold values 0 or 1
- mask_kid_top: int32 [4, 8, 4], P('parts'), parts along dimension 0, may hold values 0 or 1
- mask_kid_par: int32 [4, 4, 4], P('parts'), parts along dimension 0, may hold values 0 or 1
Outputs:
- cross_par: bfloat16 [4096, 1024], P(('parts', 'row')), parts along dimension 0
- sigma_par: bfloat16 [2048, 1024], P(('parts', 'row')), parts along dimension 0
- cross_kid_top: bfloat16 [4, 2048, 1024], P('parts', 'row'), parts along dimension 0
- cross_kid_par: bfloat16 [4, 1024, 1024], P('parts', 'row'), parts along dimension 0
- variance_kid: float32 [4, 1024], P('parts'), parts along dimension 0
There are 2 independent parts, one for each index of `parts`. A program takes and returns all parts, laid end to end along the dimension named above; each array names one. Nothing has to cross between parts.
Inputs may be any that keep to these rules, and one draw needn't show every extreme that they name: `sigma_top`: symmetric positive definite. `dinv_par`: symmetric positive definite.
All inputs are finite; a program needn't handle non-finite values.
Results may differ from a plain program's by a relative error of at most 0.0052.
Values may be sent and summed in bfloat16 or wider, within the bound.
A program may use at most 64 MiB of HBM per device.

v0:
```python
import jax
import jax.numpy as jnp
from jax import lax
from jax.sharding import PartitionSpec as P

BLK = 256


def block_mask(mask, rows, first):
    index = (first + jnp.arange(rows, dtype=jnp.int32)) // BLK
    picker = (index[:, None] == jnp.arange(mask.shape[-2], dtype=jnp.int32)[None, :]).astype(
        jnp.float32
    )
    picked = jnp.einsum("rb,...bc->...rc", picker, mask.astype(jnp.float32))
    return jnp.repeat(picked, BLK, axis=-1).astype(jnp.bfloat16)


def shards(
    sigma_top,
    panel_par,
    dinv_par,
    panel_kid_top,
    panel_kid_par,
    dvar_kid,
    mask_par,
    mask_kid_top,
    mask_kid_par,
):
    rows_top = sigma_top.shape[0]
    rows_par = dinv_par.shape[0]
    position = lax.axis_index("row")
    par_masked = panel_par * block_mask(mask_par, rows_top, position * rows_top)
    kid_top_masked = panel_kid_top * block_mask(mask_kid_top, rows_top, position * rows_top)
    kid_par_masked = panel_kid_par * block_mask(mask_kid_par, rows_par, position * rows_par)
    columns = sigma_top
    cross_wide = jnp.dot(
        columns,
        lax.all_gather(par_masked, "row", axis=0, tiled=True),
        preferred_element_type=jnp.float32,
    )
    cross_par = cross_wide.astype(jnp.bfloat16)
    turned = lax.all_to_all(par_masked, "row", split_axis=1, concat_axis=0, tiled=True)
    panel_rows = turned.T
    columns = panel_rows
    diag_sum = jnp.dot(
        columns,
        lax.all_gather(cross_par, "row", axis=0, tiled=True),
        preferred_element_type=jnp.float32,
    )
    sigma_par = (dinv_par + diag_sum).astype(jnp.bfloat16)
    turned_cross = lax.all_to_all(cross_par, "row", split_axis=1, concat_axis=0, tiled=True)
    cross_rows_par = turned_cross.T
    piece = lax.all_gather(kid_top_masked, "row", axis=1, tiled=True)
    upper = jnp.einsum("rc,kcw->krw", sigma_top, piece, preferred_element_type=jnp.float32)
    lower = jnp.einsum("rc,kcw->krw", cross_rows_par, piece, preferred_element_type=jnp.float32)
    acc_top = upper
    acc_par = lower
    piece = lax.all_gather(kid_par_masked, "row", axis=1, tiled=True)
    upper = acc_top + jnp.einsum(
        "rc,kcw->krw", cross_par, piece, preferred_element_type=jnp.float32
    )
    lower = acc_par + jnp.einsum(
        "rc,kcw->krw", sigma_par, piece, preferred_element_type=jnp.float32
    )
    cross_kid_top = upper.astype(jnp.bfloat16)
    cross_kid_par = lower.astype(jnp.bfloat16)
    partial_var = jnp.sum(
        kid_top_masked.astype(jnp.float32) * cross_kid_top.astype(jnp.float32), axis=1
    )
    partial_var = partial_var + jnp.sum(
        kid_par_masked.astype(jnp.float32) * cross_kid_par.astype(jnp.float32), axis=1
    )
    variance_kid = dvar_kid + lax.psum(partial_var, "row")
    return (cross_par, sigma_par, cross_kid_top, cross_kid_par, variance_kid)


def solution(mesh):
    return jax.shard_map(
        shards,
        mesh=mesh,
        in_specs=(
            P(("parts", "row"), None),
            P(("parts", "row"), None),
            P(("parts", "row"), None),
            P("parts", "row", None),
            P("parts", "row", None),
            P("parts", None),
            P("parts", None),
            P("parts", None, None),
            P("parts", None, None),
        ),
        out_specs=(
            P(("parts", "row"), None),
            P(("parts", "row"), None),
            P("parts", "row", None),
            P("parts", "row", None),
            P("parts", None),
        ),
        check_vma=False,
    )
```

profile of v0, /device:TPU:0, one launch (start us, length us, event | category | flops | bytes accessed | tf_op | source)
XLA Modules:
  0.0 304.0 jit_solution(11202252859310362242)
XLA Ops:
  7.3 1.2 copy.21
  8.4 0.8 convolution_convert_fusion.1
  9.2 0.7 bitcast_multiply_fusion
  10.1 55.9 %all-gather.5.cloned.1.call-done = bf16[2048,1024]{0,1:T(8,128)(2,1)} async-done(((bf16[128,1024]{0,1:T(8,128)(2,1)}), bf16[2048,1024]{0,1:T(8,128)(2,1)}) %all-gather.5.cloned.1.call-update) | async-done | bytes 4194320 | tf_op jit(solution)/shard_map/all_gather | solution.py:38
  66.0 4.1 %convolution_convert_fusion = bf16[1024,128]{1,0:T(8,128)(2,1)} fusion(bf16[2048,1024]{0,1:T(8,128)(2,1)} %all-gather.5.cloned.1.call-done, bf16[128,2048]{1,0:T(8,128)(2,1)S(1)} %copy-done), kind=kOutput, calls=%fused_computation.5 | convolution fusion | flops 537001984 | bytes 4980736 | tf_op jit(solution)/shard_map/dot_general | solution.py:36
  70.2 0.1 fusion.12
  70.3 0.1 copy.23
  70.5 0.3 broadcast_in_dim.7
  70.8 0.4 convert_element_type.81
  71.2 1.0 mul.24
  72.3 0.1 copy.24
  72.4 0.1 fusion.16
  72.6 0.1 copy.25
  72.7 0.2 broadcast_in_dim.8
  72.9 0.2 convert_element_type.85
  73.1 0.8 mul.26
  73.9 16.0 %all_to_all.38 = bf16[128,16,64]{0,2,1:T(8,128)(2,1)S(1)} all-to-all(bf16[128,16,64]{0,2,1:T(8,128)(2,1)S(1)} %bitcast.55), channel_id=1, replica_groups=mesh['parts'=2,'row'=16] {'row'}, dimensions={1} | all-to-all | bytes 524288 | tf_op jit(solution)/shard_map/all_to_all | solution.py:51
  89.9 5.7 %all-to-all-start = ((bf16[128,16,64]{0,2,1:T(8,128)(2,1)}), bf16[128,16,64]{0,2,1:T(8,128)(2,1)S(1)}, u32[]{:S(2)}, u32[]{:S(2)}) async-start(bf16[128,16,64]{0,2,1:T(8,128)(2,1)} %bitcast.2), calls=%async_computation | async-start | bytes 524288 | tf_op jit(solution)/shard_map/all_to_all | solution.py:42
  95.6 0.8 copy.28
  96.5 0.2 copy.27
  96.6 0.1 reshape.66
  96.8 9.4 %all-to-all-done = bf16[128,16,64]{0,2,1:T(8,128)(2,1)S(1)} async-done(((bf16[128,16,64]{0,2,1:T(8,128)(2,1)}), bf16[128,16,64]{0,2,1:T(8,128)(2,1)S(1)}, u32[]{:S(2)}, u32[]{:S(2)}) %all-to-all-start) | async-done | bytes 262176 | tf_op jit(solution)/shard_map/all_to_all | solution.py:42
  106.1 21.0 %all-gather.7.cloned.1.call-done = bf16[2048,1024]{0,1:T(8,128)(2,1)} async-done(((bf16[128,1024]{0,1:T(8,128)(2,1)}), bf16[2048,1024]{0,1:T(8,128)(2,1)}) %all-gather.7.cloned.1.call-update) | async-done | bytes 4194320 | tf_op jit(solution)/shard_map/all_gather | solution.py:47
  127.2 3.6 %fusion.4 = bf16[64,1024]{1,0:T(8,128)(2,1)S(1)} fusion(f32[64,1024]{1,0:T(8,128)S(1)} %copy-done.8, bf16[2048,1024]{0,1:T(8,128)(2,1)} %all-gather.7.cloned.1.call-done, bf16[128,16,64]{0,2,1:T(8,128)(2,1)S(1)} %all-to-all-done), kind=kOutput, calls=%fused_computation.8 | convolution fusion | flops 268566528 | bytes 4849664 | tf_op jit(solution)/shard_map/dot_general | solution.py:45
  130.8 73.5 %all-gather.9.cloned.1.call-done = bf16[2,2048,1024]{2,1,0:T(8,128)(2,1)} async-done(((bf16[2,128,1024]{2,1,0:T(8,128)(2,1)}), bf16[2,2048,1024]{2,1,0:T(8,128)(2,1)}) %all-gather.9.cloned.1.call-update) | async-done | bytes 8388624 | tf_op jit(solution)/shard_map/all_gather | solution.py:53
  204.3 4.6 %fusion.5 = f32[2,1024,128]{1,2,0:T(8,128)S(1)} fusion(bf16[2,2048,1024]{2,1,0:T(8,128)(2,1)} %all-gather.9.cloned.1.call-done, bf16[128,2048]{1,0:T(8,128)(2,1)S(1)} %copy-done), kind=kOutput, calls=%fused_computation.11 | convolution fusion | flops 1073741824 | bytes 9961472 | tf_op jit(solution)/shard_map/rc,kcw->krw/dot_general | solution.py:54
  209.0 46.4 %all-gather.11.cloned.1.call-done = bf16[2,1024,1024]{2,1,0:T(8,128)(2,1)} async-done(((bf16[2,64,1024]{2,1,0:T(8,128)(2,1)}), bf16[2,1024,1024]{2,1,0:T(8,128)(2,1)}) %all-gather.11.cloned.1.call-update) | async-done | bytes 4194320 | tf_op jit(solution)/shard_map/all_gather | solution.py:58
  255.4 3.2 %fusion.10 = f32[2,1024,64]{1,2,0:T(8,128)S(1)} fusion(bf16[2,1024,1024]{2,1,0:T(8,128)(2,1)} %all-gather.11.cloned.1.call-done, bf16[64,1024]{1,0:T(8,128)(2,1)S(1)} %fusion.4), kind=kOutput, calls=%fused_computation.18 | convolution fusion | flops 268435456 | bytes 4849664 | tf_op jit(solution)/shard_map/rc,kcw->krw/dot_general | solution.py:62
  258.6 4.2 %multiply_reduce_fusion = (f32[2,1024]{1,0:T(2,128)S(1)}, bf16[2,128,1024]{2,1,0:T(8,128)(2,1)}) fusion(bf16[2,128,1024]{2,1,0:T(8,128)(2,1)S(1)} %copy-done.2, f32[2,1024,128]{1,2,0:T(8,128)S(1)} %fusion.5, bf16[2,1024,1024]{2,1,0:T(8,128)(2,1)} %all-gather.11.cloned.1.call-done, bf16[1024,128]{1,0:T(8,128)(2,1)S(1)} %copy-done.4), kind=kOutput, calls=%fused_computation.10 | convolution fusion | flops 538441728 | bytes 6561792 | tf_op jit(solution)/shard_map/rc,kcw->krw/dot_general | solution.py:59
  262.8 2.3 multiply_reduce_fusion.1
  265.1 31.7 %psum.7 = f32[2,1024]{1,0:T(2,128)S(1)} all-reduce(f32[2,1024]{1,0:T(2,128)S(1)} %add.58), channel_id=1, replica_groups=mesh['parts'=2,'row'=16] {'row'}, use_global_device_ids=true, to_apply=%region_2.3 | all-reduce | flops 2048 | bytes 16384 | tf_op jit(solution)/shard_map/psum | solution.py:73
  296.8 0.6 add.59
  (39 shorter events, 0.3 us)
Async XLA Ops:
  7.2 58.8 %copy-start = (bf16[128,2048]{1,0:T(8,128)(2,1)S(1)}, bf16[128,2048]{1,0:T(8,128)(2,1)}, u32[]{:S(2)}) copy-start(bf16[128,2048]{1,0:T(8,128)(2,1)} %param.9) | copy-start | bytes 1572868
  7.2 63.0 %copy-start.10 = (s32[2,8,4]{1,2,0:T(4,128)S(1)}, s32[2,8,4]{1,2,0:T(4,128)}, u32[]{:S(2)}) copy-start(s32[2,8,4]{1,2,0:T(4,128)} %param.16) | copy-start | bytes 772
  7.2 58.8 %all-gather.5.cloned.1.call-start = ((), (), s32[]{:S(2)}) async-start(), calls=%async_computation.2 | async-start | bytes 4456448 | tf_op jit(solution)/shard_map/all_gather | solution.py:38
  10.0 61.2 %copy-start.5 = (bf16[2,128,1024]{2,1,0:T(8,128)(2,1)S(1)}, bf16[2,128,1024]{2,1,0:T(8,128)(2,1)}, u32[]{:S(2)}) copy-start(bf16[2,128,1024]{2,1,0:T(8,128)(2,1)} %param.12) | copy-start | bytes 1572868
  10.0 62.3 %copy-start.11 = (s32[2,4,4]{2,1,0:T(4,128)S(1)}, s32[2,4,4]{2,1,0:T(4,128)}, u32[]{:S(2)}) copy-start(s32[2,4,4]{2,1,0:T(4,128)} %param.17) | copy-start | bytes 388
  10.0 63.1 %copy-start.7 = (bf16[2,64,1024]{2,1,0:T(8,128)(2,1)S(1)}, bf16[2,64,1024]{2,1,0:T(8,128)(2,1)}, u32[]{:S(2)}) copy-start(bf16[2,64,1024]{2,1,0:T(8,128)(2,1)} %param.13) | copy-start | bytes 786436
  10.0 117.2 %all-gather.7.cloned.1.call-start = ((), (), s32[]{:S(2)}) async-start(), calls=%async_computation.3 | async-start | bytes 4456448 | tf_op jit(solution)/shard_map/all_gather | solution.py:47
  70.1 3.8 %copy-start.4 = (bf16[1024,128]{1,0:T(8,128)(2,1)S(1)}, bf16[1024,128]{1,0:T(8,128)(2,1)}, u32[]{:S(2)}) copy-start(bf16[1024,128]{1,0:T(8,128)(2,1)} %convolution_convert_fusion) | copy-start | bytes 786436
  70.1 134.2 %all-gather.9.cloned.1.call-start = ((), (), s32[]{:S(2)}) async-start(), calls=%async_computation.4 | async-start | bytes 8912896 | tf_op jit(solution)/shard_map/all_gather | solution.py:53
  70.2 57.0 %copy-start.8 = (f32[64,1024]{1,0:T(8,128)S(1)}, f32[64,1024]{1,0:T(8,128)}, u32[]{:S(2)}) copy-start(f32[64,1024]{1,0:T(8,128)} %param.11) | copy-start | bytes 786436
  72.2 183.1 %all-gather.11.cloned.1.call-start = ((), (), s32[]{:S(2)}) async-start(), calls=%async_computation.5 | async-start | bytes 4456448 | tf_op jit(solution)/shard_map/all_gather | solution.py:58
  89.9 16.3 %all-to-all-start = ((bf16[128,16,64]{0,2,1:T(8,128)(2,1)}), bf16[128,16,64]{0,2,1:T(8,128)(2,1)S(1)}, u32[]{:S(2)}, u32[]{:S(2)}) async-start(bf16[128,16,64]{0,2,1:T(8,128)(2,1)} %bitcast.2), calls=%async_computation | async-start | bytes 524288 | tf_op jit(solution)/shard_map/all_to_all | solution.py:42
  130.8 124.6 %copy-start.6 = (bf16[64,1024]{1,0:T(8,128)(2,1)}, bf16[64,1024]{1,0:T(8,128)(2,1)S(1)}, u32[]{:S(2)}) copy-start(bf16[64,1024]{1,0:T(8,128)(2,1)S(1)} %fusion.4) | copy-start | bytes 393220
  208.9 49.6 %copy-start.2 = (bf16[2,128,1024]{2,1,0:T(8,128)(2,1)S(1)}, bf16[2,128,1024]{2,1,0:T(8,128)(2,1)}, u32[]{:S(2)}) copy-start(bf16[2,128,1024]{2,1,0:T(8,128)(2,1)} %mul.24) | copy-start | bytes 1572868
  255.4 7.4 %copy-start.1 = (bf16[2,2048,1024]{2,1,0:T(8,128)(2,1)S(1)}, bf16[2,2048,1024]{2,1,0:T(8,128)(2,1)}, u32[]{:S(2)}) copy-start(bf16[2,2048,1024]{2,1,0:T(8,128)(2,1)} %all-gather.9.cloned.1.call-done) | copy-start | bytes 25165828
  258.6 4.3 %copy-start.3 = (bf16[2,64,1024]{2,1,0:T(8,128)(2,1)S(1)}, bf16[2,64,1024]{2,1,0:T(8,128)(2,1)}, u32[]{:S(2)}) copy-start(bf16[2,64,1024]{2,1,0:T(8,128)(2,1)} %mul.26) | copy-start | bytes 786436
  262.8 34.0 %copy-start.9 = (f32[2,1024]{1,0:T(2,128)S(1)}, f32[2,1024]{1,0:T(2,128)}, u32[]{:S(2)}) copy-start(f32[2,1024]{1,0:T(2,128)} %param.14) | copy-start | bytes 24580
Sparse Core Ops, SparseCore 0:
  10.7 55.1 all-gather.4
  70.2 56.9 all-gather.6
  130.0 74.2 all-gather.8
  206.3 48.9 all-gather.10
where the time goes:
time: 304 us
  waiting for transfers between devices  206 us (68%)
  blocking collectives  47.7 us (16%)
  matrix products  23.1 us (8%)
  between operations  14 us (5%)
  starting transfers between devices  5.89 us (2%)
  local copies, waits for them, and re-layouts  3.83 us (1%)
  other arithmetic  3.14 us (1%)
    all_gather x1, waiting for transfers between devices, shards(): piece = lax.all_gather(kid_top_masked, 'row', axis=1, tiled=True)  73.5 us
    all_gather x1, waiting for transfers between devices, shards(): lax.all_gather(par_masked, 'row', axis=0, tiled=True)  55.9 us
    all_gather x1, waiting for transfers between devices, shards(): piece = lax.all_gather(kid_par_masked, 'row', axis=1, tiled=True)  46.4 us
    psum x1, blocking collectives, shards(): variance_kid = dvar_kid + lax.psum(partial_var, 'row')  31.7 us
    all_gather x1, waiting for transfers between devices, shards(): lax.all_gather(cross_par, 'row', axis=0, tiled=True)  21 us
    all_to_all x1, blocking collectives, shards(): lax.all_to_all(cross_par, 'row', split_axis=1, concat_axis=0, tiled=True)  16 us
    all_to_all x1, waiting for transfers between devices, shards(): lax.all_to_all(par_masked, 'row', split_axis=1, concat_axis=0, tiled=True)  9.39 us
  transfers between devices with their start and end apart: 5, of which 5 were waited for; matrix products, arithmetic and copies ran while one was open for 4% of the time, Pallas kernels for 0%

commit v1 on v0

--- a/solution.py
+++ b/solution.py
@@ -4,6 +4,10 @@
 from jax.sharding import PartitionSpec as P
 
 BLK = 256
+
+
+def guide_values_now(sample, axis_name):
+    return jnp.sum(lax.all_gather(sample, axis_name), 0)
 
 
 def block_mask(mask, rows, first):
@@ -70,7 +74,7 @@
     partial_var = partial_var + jnp.sum(
         kid_par_masked.astype(jnp.float32) * cross_kid_par.astype(jnp.float32), axis=1
     )
-    variance_kid = dvar_kid + lax.psum(partial_var, "row")
+    variance_kid = dvar_kid + guide_values_now(partial_var, "row")
     return (cross_par, sigma_par, cross_kid_top, cross_kid_par, variance_kid)
 
 

time: 304 us -> 292 us (0.961)
  blocking collectives: 47.7 us -> 35.3 us
    psum x1 -> x0, blocking collectives: 31.7 us -> none  [shards(): variance_kid = dvar_kid + lax.psum(partial_var, 'row')]
    all_gather x0 -> x1, blocking collectives: none -> 19.3 us  [guide_values_now(): return jnp.sum(lax.all_gather(sample, axis_name), 0)]
where the time goes in v1:
time: 292 us
  waiting for transfers between devices  206 us (71%)
  blocking collectives  35.3 us (12%)
  matrix products  23.1 us (8%)
  between operations  14 us (5%)
  starting transfers between devices  5.89 us (2%)
  local copies, waits for them, and re-layouts  3.83 us (1%)
  other arithmetic  3.2 us (1%)
    all_gather x1, waiting for transfers between devices, shards(): piece = lax.all_gather(kid_top_masked, 'row', axis=1, tiled=True)  73.5 us
    all_gather x1, waiting for transfers between devices, shards(): lax.all_gather(par_masked, 'row', axis=0, tiled=True)  55.9 us
    all_gather x1, waiting for transfers between devices, shards(): piece = lax.all_gather(kid_par_masked, 'row', axis=1, tiled=True)  46.4 us
    all_gather x1, waiting for transfers between devices, shards(): lax.all_gather(cross_par, 'row', axis=0, tiled=True)  21 us
    all_gather x1, blocking collectives, guide_values_now(): return jnp.sum(lax.all_gather(sample, axis_name), 0)  19.3 us
    all_to_all x1, blocking collectives, shards(): lax.all_to_all(cross_par, 'row', split_axis=1, concat_axis=0, tiled=True)  16 us
    all_to_all x1, waiting for transfers between devices, shards(): lax.all_to_all(par_masked, 'row', split_axis=1, concat_axis=0, tiled=True)  9.39 us
  transfers between devices with their start and end apart: 5, of which 5 were waited for; matrix products, arithmetic and copies ran while one was open for 4% of the time, Pallas kernels for 0%

profile of v1, /device:TPU:0, one launch (start us, length us, event | category | flops | bytes accessed | tf_op | source)
XLA Modules:
  0.0 291.6 jit_solution(232374125042991005)
XLA Ops:
  7.3 1.2 copy.29
  8.4 0.8 convolution_convert_fusion.1
  9.2 0.7 bitcast_multiply_fusion
  10.1 55.9 %all-gather.7.cloned.1.call-done = bf16[2048,1024]{0,1:T(8,128)(2,1)} async-done(((bf16[128,1024]{0,1:T(8,128)(2,1)}), bf16[2048,1024]{0,1:T(8,128)(2,1)}) %all-gather.7.cloned.1.call-update) | async-done | bytes 4194320 | tf_op jit(solution)/shard_map/all_gather | solution.py:42
  66.0 4.1 %convolution_convert_fusion = bf16[1024,128]{1,0:T(8,128)(2,1)} fusion(bf16[2048,1024]{0,1:T(8,128)(2,1)} %all-gather.7.cloned.1.call-done, bf16[128,2048]{1,0:T(8,128)(2,1)S(1)} %copy-done), kind=kOutput, calls=%fused_computation.5 | convolution fusion | flops 537001984 | bytes 4980736 | tf_op jit(solution)/shard_map/dot_general | solution.py:40
  70.2 0.1 fusion.12
  70.3 0.1 copy.31
  70.5 0.3 broadcast_in_dim.7
  70.8 0.4 convert_element_type.81
  71.2 1.0 mul.24
  72.3 0.1 copy.32
  72.4 0.1 fusion.16
  72.6 0.1 copy.33
  72.7 0.2 broadcast_in_dim.8
  72.9 0.2 convert_element_type.85
  73.1 0.8 mul.26
  73.9 16.0 %all_to_all.38 = bf16[128,16,64]{0,2,1:T(8,128)(2,1)S(1)} all-to-all(bf16[128,16,64]{0,2,1:T(8,128)(2,1)S(1)} %bitcast.57), channel_id=1, replica_groups=mesh['parts'=2,'row'=16] {'row'}, dimensions={1} | all-to-all | bytes 524288 | tf_op jit(solution)/shard_map/all_to_all | solution.py:55
  89.9 5.7 %all-to-all-start = ((bf16[128,16,64]{0,2,1:T(8,128)(2,1)}), bf16[128,16,64]{0,2,1:T(8,128)(2,1)S(1)}, u32[]{:S(2)}, u32[]{:S(2)}) async-start(bf16[128,16,64]{0,2,1:T(8,128)(2,1)} %bitcast.2), calls=%async_computation | async-start | bytes 524288 | tf_op jit(solution)/shard_map/all_to_all | solution.py:46
  95.6 0.8 copy.36
  96.5 0.2 copy.35
  96.6 0.1 reshape.82
  96.8 9.4 %all-to-all-done = bf16[128,16,64]{0,2,1:T(8,128)(2,1)S(1)} async-done(((bf16[128,16,64]{0,2,1:T(8,128)(2,1)}), bf16[128,16,64]{0,2,1:T(8,128)(2,1)S(1)}, u32[]{:S(2)}, u32[]{:S(2)}) %all-to-all-start) | async-done | bytes 262176 | tf_op jit(solution)/shard_map/all_to_all | solution.py:46
  106.1 21.0 %all-gather.9.cloned.1.call-done = bf16[2048,1024]{0,1:T(8,128)(2,1)} async-done(((bf16[128,1024]{0,1:T(8,128)(2,1)}), bf16[2048,1024]{0,1:T(8,128)(2,1)}) %all-gather.9.cloned.1.call-update) | async-done | bytes 4194320 | tf_op jit(solution)/shard_map/all_gather | solution.py:51
  127.2 3.6 %fusion.4 = bf16[64,1024]{1,0:T(8,128)(2,1)S(1)} fusion(f32[64,1024]{1,0:T(8,128)S(1)} %copy-done.8, bf16[2048,1024]{0,1:T(8,128)(2,1)} %all-gather.9.cloned.1.call-done, bf16[128,16,64]{0,2,1:T(8,128)(2,1)S(1)} %all-to-all-done), kind=kOutput, calls=%fused_computation.8 | convolution fusion | flops 268566528 | bytes 4849664 | tf_op jit(solution)/shard_map/dot_general | solution.py:49
  130.8 73.5 %all-gather.11.cloned.1.call-done = bf16[2,2048,1024]{2,1,0:T(8,128)(2,1)} async-done(((bf16[2,128,1024]{2,1,0:T(8,128)(2,1)}), bf16[2,2048,1024]{2,1,0:T(8,128)(2,1)}) %all-gather.11.cloned.1.call-update) | async-done | bytes 8388624 | tf_op jit(solution)/shard_map/all_gather | solution.py:57
  204.3 4.6 %fusion.5 = f32[2,1024,128]{1,2,0:T(8,128)S(1)} fusion(bf16[2,2048,1024]{2,1,0:T(8,128)(2,1)} %all-gather.11.cloned.1.call-done, bf16[128,2048]{1,0:T(8,128)(2,1)S(1)} %copy-done), kind=kOutput, calls=%fused_computation.11 | convolution fusion | flops 1073741824 | bytes 9961472 | tf_op jit(solution)/shard_map/rc,kcw->krw/dot_general | solution.py:58
  209.0 46.4 %all-gather.13.cloned.1.call-done = bf16[2,1024,1024]{2,1,0:T(8,128)(2,1)} async-done(((bf16[2,64,1024]{2,1,0:T(8,128)(2,1)}), bf16[2,1024,1024]{2,1,0:T(8,128)(2,1)}) %all-gather.13.cloned.1.call-update) | async-done | bytes 4194320 | tf_op jit(solution)/shard_map/all_gather | solution.py:62
  255.4 3.2 %fusion.10 = f32[2,1024,64]{1,2,0:T(8,128)S(1)} fusion(bf16[2,1024,1024]{2,1,0:T(8,128)(2,1)} %all-gather.13.cloned.1.call-done, bf16[64,1024]{1,0:T(8,128)(2,1)S(1)} %fusion.4), kind=kOutput, calls=%fused_computation.18 | convolution fusion | flops 268435456 | bytes 4849664 | tf_op jit(solution)/shard_map/rc,kcw->krw/dot_general | solution.py:66
  258.6 4.2 %multiply_reduce_fusion = (f32[2,1024]{1,0:T(2,128)S(1)}, bf16[2,128,1024]{2,1,0:T(8,128)(2,1)}) fusion(bf16[2,128,1024]{2,1,0:T(8,128)(2,1)S(1)} %copy-done.2, f32[2,1024,128]{1,2,0:T(8,128)S(1)} %fusion.5, bf16[2,1024,1024]{2,1,0:T(8,128)(2,1)} %all-gather.13.cloned.1.call-done, bf16[1024,128]{1,0:T(8,128)(2,1)S(1)} %copy-done.4), kind=kOutput, calls=%fused_computation.10 | convolution fusion | flops 538441728 | bytes 6561792 | tf_op jit(solution)/shard_map/rc,kcw->krw/dot_general | solution.py:63
  262.8 2.3 multiply_reduce_fusion.1
  265.1 19.3 %all-gather.1 = f32[16,2,1024]{2,1,0:T(2,128)S(1)} all-gather(f32[1,2,1024]{2,1,0:T(2,128)S(1)} %add_bitcast_fusion), channel_id=2, replica_groups=mesh['parts'=2,'row'=16] {'row'}, dimensions={0}, use_global_device_ids=true | all-gather | bytes 139264 | tf_op jit(solution)/shard_map/all_gather | solution.py:10
  284.5 0.6 add.68
  (40 shorter events, 0.4 us)
Async XLA Ops:
  7.2 58.8 %copy-start = (bf16[128,2048]{1,0:T(8,128)(2,1)S(1)}, bf16[128,2048]{1,0:T(8,128)(2,1)}, u32[]{:S(2)}) copy-start(bf16[128,2048]{1,0:T(8,128)(2,1)} %param.9) | copy-start | bytes 1572868
  7.2 63.0 %copy-start.10 = (s32[2,8,4]{1,2,0:T(4,128)S(1)}, s32[2,8,4]{1,2,0:T(4,128)}, u32[]{:S(2)}) copy-start(s32[2,8,4]{1,2,0:T(4,128)} %param.16) | copy-start | bytes 772
  7.2 58.8 %all-gather.7.cloned.1.call-start = ((), (), s32[]{:S(2)}) async-start(), calls=%async_computation.2 | async-start | bytes 4456448 | tf_op jit(solution)/shard_map/all_gather | solution.py:42
  10.0 61.2 %copy-start.5 = (bf16[2,128,1024]{2,1,0:T(8,128)(2,1)S(1)}, bf16[2,128,1024]{2,1,0:T(8,128)(2,1)}, u32[]{:S(2)}) copy-start(bf16[2,128,1024]{2,1,0:T(8,128)(2,1)} %param.12) | copy-start | bytes 1572868
  10.0 62.3 %copy-start.11 = (s32[2,4,4]{2,1,0:T(4,128)S(1)}, s32[2,4,4]{2,1,0:T(4,128)}, u32[]{:S(2)}) copy-start(s32[2,4,4]{2,1,0:T(4,128)} %param.17) | copy-start | bytes 388
  10.0 63.1 %copy-start.7 = (bf16[2,64,1024]{2,1,0:T(8,128)(2,1)S(1)}, bf16[2,64,1024]{2,1,0:T(8,128)(2,1)}, u32[]{:S(2)}) copy-start(bf16[2,64,1024]{2,1,0:T(8,128)(2,1)} %param.13) | copy-start | bytes 786436
  10.0 117.2 %all-gather.9.cloned.1.call-start = ((), (), s32[]{:S(2)}) async-start(), calls=%async_computation.3 | async-start | bytes 4456448 | tf_op jit(solution)/shard_map/all_gather | solution.py:51
  70.1 3.8 %copy-start.4 = (bf16[1024,128]{1,0:T(8,128)(2,1)S(1)}, bf16[1024,128]{1,0:T(8,128)(2,1)}, u32[]{:S(2)}) copy-start(bf16[1024,128]{1,0:T(8,128)(2,1)} %convolution_convert_fusion) | copy-start | bytes 786436
  70.1 134.2 %all-gather.11.cloned.1.call-start = ((), (), s32[]{:S(2)}) async-start(), calls=%async_computation.4 | async-start | bytes 8912896 | tf_op jit(solution)/shard_map/all_gather | solution.py:57
  70.2 57.0 %copy-start.8 = (f32[64,1024]{1,0:T(8,128)S(1)}, f32[64,1024]{1,0:T(8,128)}, u32[]{:S(2)}) copy-start(f32[64,1024]{1,0:T(8,128)} %param.11) | copy-start | bytes 786436
  72.2 183.1 %all-gather.13.cloned.1.call-start = ((), (), s32[]{:S(2)}) async-start(), calls=%async_computation.5 | async-start | bytes 4456448 | tf_op jit(solution)/shard_map/all_gather | solution.py:62
  89.9 16.3 %all-to-all-start = ((bf16[128,16,64]{0,2,1:T(8,128)(2,1)}), bf16[128,16,64]{0,2,1:T(8,128)(2,1)S(1)}, u32[]{:S(2)}, u32[]{:S(2)}) async-start(bf16[128,16,64]{0,2,1:T(8,128)(2,1)} %bitcast.2), calls=%async_computation | async-start | bytes 524288 | tf_op jit(solution)/shard_map/all_to_all | solution.py:46
  130.8 124.6 %copy-start.6 = (bf16[64,1024]{1,0:T(8,128)(2,1)}, bf16[64,1024]{1,0:T(8,128)(2,1)S(1)}, u32[]{:S(2)}) copy-start(bf16[64,1024]{1,0:T(8,128)(2,1)S(1)} %fusion.4) | copy-start | bytes 393220
  208.9 49.6 %copy-start.2 = (bf16[2,128,1024]{2,1,0:T(8,128)(2,1)S(1)}, bf16[2,128,1024]{2,1,0:T(8,128)(2,1)}, u32[]{:S(2)}) copy-start(bf16[2,128,1024]{2,1,0:T(8,128)(2,1)} %mul.24) | copy-start | bytes 1572868
  255.4 7.4 %copy-start.1 = (bf16[2,2048,1024]{2,1,0:T(8,128)(2,1)S(1)}, bf16[2,2048,1024]{2,1,0:T(8,128)(2,1)}, u32[]{:S(2)}) copy-start(bf16[2,2048,1024]{2,1,0:T(8,128)(2,1)} %all-gather.11.cloned.1.call-done) | copy-start | bytes 25165828
  258.6 4.3 %copy-start.3 = (bf16[2,64,1024]{2,1,0:T(8,128)(2,1)S(1)}, bf16[2,64,1024]{2,1,0:T(8,128)(2,1)}, u32[]{:S(2)}) copy-start(bf16[2,64,1024]{2,1,0:T(8,128)(2,1)} %mul.26) | copy-start | bytes 786436
  262.8 21.7 %copy-start.9 = (f32[2,1024]{1,0:T(2,128)S(1)}, f32[2,1024]{1,0:T(2,128)}, u32[]{:S(2)}) copy-start(f32[2,1024]{1,0:T(2,128)} %param.14) | copy-start | bytes 24580
Sparse Core Ops, SparseCore 0:
  10.7 55.1 all-gather.6
  70.2 56.9 all-gather.8
  130.0 74.2 all-gather.10
  206.3 48.9 all-gather.12
